TPU v7x, 32 devices: a whole 2x2x4 slice. The times are simulated.
32 devices in a mesh: dp: 4 (over y, core), tensor: 8 (over z, x).
Axes of the slice: x: 2, y: 2, z: 4, core: 2. Of those that a mesh axis runs over, the one named last changes fastest.
Arguments:
- query_latent: bfloat16 [64, 1536], P(('dp', 'tensor')), may hold values from -40 to 40
- key_value_latent: bfloat16 [64, 512], P(('dp', 'tensor')), may hold values from -40 to 40
- query_gain: float32 [1536], replicated, may hold values from 0.5 to 1.5
- key_value_gain: float32 [512], replicated, may hold values from 0.5 to 1.5
- q_up: bfloat16 [1536, 3072], P(None, 'tensor'), may hold values from -0.625 to 0.625
- kv_up: bfloat16 [512, 4096], P(None, 'tensor'), may hold values from -1 to 1
- grad_q: bfloat16 [64, 3072], P('dp', 'tensor'), may hold values from -0.23925781 to 0.23925781
- grad_kv: bfloat16 [64, 4096], P('dp', 'tensor'), may hold values from -0.23925781 to 0.23925781
Outputs:
- query_latent_gradient: float32 [64, 1536], P(('dp', 'tensor'))
- key_value_latent_gradient: float32 [64, 512], P(('dp', 'tensor'))
- d_q_up: float32 [1536, 3072], P('dp', 'tensor')
- d_kv_up: float32 [512, 4096], P('dp', 'tensor')
All inputs are finite; a program needn't handle non-finite values.
Results may differ from a plain program's by a relative error of at most 0.0029.
Values may be sent and summed in bfloat16 or wider, within the bound.
No kernel may reach another device: no remote copies, remote signals or barrier semaphores. Data moves between devices by JAX's collectives and lax.ppermute only.
A program may use at most 64 MiB of HBM per device.

v0:
```python
import jax
import jax.numpy as jnp
from jax import lax
from jax.sharding import PartitionSpec as P

EPS = 1e-06


def apply_norm(raw, norm_gain):
    input_values = raw.astype(jnp.float32)
    inverse_norm = lax.rsqrt(jnp.mean(input_values * input_values, axis=-1, keepdims=True) + EPS)
    unit_input = input_values * inverse_norm
    return (unit_input, inverse_norm, (norm_gain * unit_input).astype(jnp.bfloat16))


def backward_of_norm(incoming_gradient, unit_input, inverse_norm, norm_gain):
    scaled_gradient = norm_gain * incoming_gradient
    mean_correction = jnp.mean(scaled_gradient * unit_input, axis=-1, keepdims=True)
    return inverse_norm * (scaled_gradient - unit_input * mean_correction)


def contract_rows(left, right):
    return lax.dot_general(
        left, right, (((0,), (0,)), ((), ())), preferred_element_type=jnp.float32
    )


def contract_cols(left, right):
    return lax.dot_general(
        left, right, (((1,), (1,)), ((), ())), preferred_element_type=jnp.float32
    )


def body(query_latent, key_value_latent, query_gain, key_value_gain, q_up, kv_up, grad_q, grad_kv):
    query_width = query_latent.shape[1]
    whole_q, whole_kv = (
        lax.all_gather(query_latent, "tensor", axis=0, tiled=True),
        lax.all_gather(key_value_latent, "tensor", axis=0, tiled=True),
    )
    part_q = contract_rows(apply_norm(whole_q, query_gain)[2], grad_q)
    part_kv = contract_rows(apply_norm(whole_kv, key_value_gain)[2], grad_kv)
    d_q_up, d_kv_up = (
        lax.psum_scatter(part_q, "dp", scatter_dimension=0, tiled=True),
        lax.psum_scatter(part_kv, "dp", scatter_dimension=0, tiled=True),
    )
    summed_products = lax.psum_scatter(
        jnp.concatenate((contract_cols(grad_q, q_up), contract_cols(grad_kv, kv_up)), axis=1),
        "tensor",
        scatter_dimension=0,
        tiled=True,
    )
    query_unit, query_inverse_norm, unused_item = apply_norm(query_latent, query_gain)
    key_value_unit, key_value_inverse_norm, unused_item = apply_norm(
        key_value_latent, key_value_gain
    )
    query_latent_gradient = backward_of_norm(
        summed_products[:, :query_width], query_unit, query_inverse_norm, query_gain
    )
    key_value_latent_gradient = backward_of_norm(
        summed_products[:, query_width:], key_value_unit, key_value_inverse_norm, key_value_gain
    )
    return (query_latent_gradient, key_value_latent_gradient, d_q_up, d_kv_up)


def solution(mesh):
    return jax.shard_map(
        body,
        mesh=mesh,
        in_specs=(
            P(("dp", "tensor"), None),
            P(("dp", "tensor"), None),
            P(),
            P(),
            P(None, "tensor"),
            P(None, "tensor"),
            P("dp", "tensor"),
            P("dp", "tensor"),
        ),
        out_specs=(
            P(("dp", "tensor"), None),
            P(("dp", "tensor"), None),
            P("dp", "tensor"),
            P("dp", "tensor"),
        ),
        check_vma=False,
    )
```

profile of v0, /device:TPU:0, one launch (start us, length us, event | category | flops | bytes accessed | tf_op | source)
XLA Modules:
  0.0 113.6 jit_solution(14444127462413539571)
XLA Ops:
  8.0 0.0 copy-start
  8.1 0.0 all-reduce.3.cloned.1.call-start
  8.1 1.2 %copy-done = bf16[1536,384]{1,0:T(8,128)(2,1)S(1)} copy-done((bf16[1536,384]{1,0:T(8,128)(2,1)S(1)}, bf16[1536,384]{1,0:T(8,128)(2,1)}, u32[]{:S(2)}) %copy-start) | copy-done | bytes 1179672
  9.3 1.1 fusion.18
  10.4 0.0 copy-done.4
  10.4 0.3 fusion.19
  10.6 0.7 pad_maximum_fusion
  11.3 0.0 all-reduce.3.cloned.1.call-update
  11.3 0.0 reduce-scatter.5.cloned.1.call-start
  11.4 27.9 %all-gather.1 = bf16[8,2,512]{2,1,0:T(2,128)(2,1)S(1)} all-gather(bf16[1,2,512]{2,1,0:T(2,128)(2,1)S(1)} %bitcast.10), channel_id=1, replica_groups=mesh['dp'=4,'tensor'=8] {'tensor'}, dimensions={0}, use_global_device_ids=true | all-gather | bytes 18432 | tf_op jit(solution)/shard_map/all_gather | solution.py:38
  39.3 0.1 multiply_reduce_fusion.1
  39.5 0.0 copy-done.7
  39.5 0.0 copy-start.3
  39.5 0.0 copy-start.5
  39.5 1.4 %fusion.3 = f32[512,512]{1,0:T(8,128)} fusion(bf16[16,512]{1,0:T(8,128)(2,1)S(1)} %copy-done.4, f32[16,512]{1,0:T(8,128)S(1)} %reshape.55, f32[16]{0:T(128)S(1)} %add_rsqrt_fusion, f32[512]{0:T(512)S(1)} %copy-done.7), kind=kOutput, calls=%fused_computation.8 | convolution fusion | flops 8413184 | bytes 1099840 | tf_op jit(solution)/shard_map/dot_general | solution.py:23
  40.9 0.0 reduce-scatter.5.cloned.1.call-update
  40.9 0.0 reduce-scatter.3.cloned.1.call-start
  41.0 30.8 %all-gather = bf16[8,2,1536]{2,1,0:T(2,128)(2,1)S(1)} all-gather(bf16[1,2,1536]{2,1,0:T(2,128)(2,1)S(1)} %bitcast.9), channel_id=1, replica_groups=mesh['dp'=4,'tensor'=8] {'tensor'}, dimensions={0}, use_global_device_ids=true | all-gather | bytes 55296 | tf_op jit(solution)/shard_map/all_gather | solution.py:37
  71.8 0.1 multiply_reduce_fusion
  71.9 0.0 copy-done.5
  71.9 2.0 %fusion = f32[1536,384]{1,0:T(8,128)} fusion(bf16[16,384]{1,0:T(8,128)(2,1)S(1)} %copy-done.5, f32[16,1536]{1,0:T(8,128)S(1)} %reshape.54, f32[16]{0:T(128)S(1)} %add_rsqrt_fusion.1, f32[1536]{0:T(1024)S(1)} %copy-done.3), kind=kOutput, calls=%fused_computation.3 | convolution fusion | flops 18948096 | bytes 2476096 | tf_op jit(solution)/shard_map/dot_general | solution.py:23
  73.9 0.0 reduce-scatter.3.cloned.1.call-update
  73.9 0.6 copy-done.8
  74.6 0.6 dynamic-slice
  75.8 0.1 fusion.17
  75.9 0.1 fusion.11
  76.1 9.4 %all-reduce.3.cloned.1.call-done = f32[16,2048]{1,0:T(8,128)} async-done(((f32[16,2048]{1,0:T(8,128)}), f32[16,2048]{1,0:T(8,128)}) %all-reduce.3.cloned.1.call-update) | async-done | bytes 131088
  85.5 0.9 fusion.14
  86.4 1.0 fusion.8
  87.4 1.4 %fusion.16 = f32[2,512]{1,0:T(2,128)} fusion(bf16[2,512]{1,0:T(2,128)(2,1)S(1)} %copy-done.6, f32[2]{0:T(128)S(1)} %broadcast_multiply_fusion, f32[2]{0:T(128)S(1)} %add_rsqrt_fusion.2, f32[16,2048]{1,0:T(8,128)} %all-reduce.3.cloned.1.call-done, u32[]{:T(128)S(6)} %multiply.37, u32[]{:T(128)S(6)} %convert, f32[512]{0:T(512)S(1)} %copy-done.7), kind=kLoop, calls=%fused_computation.26 | loop fusion | flops 6144 | bytes 12312 | tf_op jit(solution)/shard_map/mul | solution.py:19
  88.8 1.5 %fusion.10 = f32[2,1536]{1,0:T(2,128)} fusion(bf16[2,1536]{1,0:T(2,128)(2,1)S(1)} %copy-done.2, f32[16,2048]{1,0:T(8,128)} %all-reduce.3.cloned.1.call-done, u32[]{:T(128)S(6)} %multiply.37, f32[2]{0:T(128)S(1)} %broadcast_multiply_fusion.1, f32[2]{0:T(128)S(1)} %add_rsqrt_fusion.3, f32[1536]{0:T(1024)S(1)} %copy-done.3), kind=kLoop, calls=%fused_computation.17 | loop fusion | flops 18432 | bytes 36884 | tf_op jit(solution)/shard_map/mul | solution.py:19
  90.3 15.9 %reduce-scatter.3.cloned.1.call-done = f32[384,384]{1,0:T(8,128)} async-done(((f32[1536,384]{1,0:T(8,128)}), f32[384,384]{1,0:T(8,128)}) %reduce-scatter.3.cloned.1.call-update) | async-done | bytes 589840 | tf_op jit(solution)/shard_map/reduce_scatter | solution.py:43
  (19 shorter events, 0.1 us)
Async XLA Ops:
  8.0 1.3 %copy-start = (bf16[1536,384]{1,0:T(8,128)(2,1)S(1)}, bf16[1536,384]{1,0:T(8,128)(2,1)}, u32[]{:S(2)}) copy-start(bf16[1536,384]{1,0:T(8,128)(2,1)} %param.12) | copy-start | bytes 3538948
  8.0 2.4 %copy-start.1 = (bf16[512,512]{1,0:T(8,128)(2,1)S(1)}, bf16[512,512]{1,0:T(8,128)(2,1)}, u32[]{:S(2)}) copy-start(bf16[512,512]{1,0:T(8,128)(2,1)} %param.13) | copy-start | bytes 1572868
  8.0 2.4 %copy-start.4 = (bf16[16,512]{1,0:T(8,128)(2,1)S(1)}, bf16[16,512]{1,0:T(8,128)(2,1)}, u32[]{:S(2)}) copy-start(bf16[16,512]{1,0:T(8,128)(2,1)} %param.15) | copy-start | bytes 49156
  8.0 3.4 %copy-start.6 = (bf16[2,512]{1,0:T(2,128)(2,1)S(1)}, bf16[2,512]{1,0:T(2,128)(2,1)}, u32[]{:S(2)}) copy-start(bf16[2,512]{1,0:T(2,128)(2,1)} %param.9) | copy-start | bytes 6148
  8.0 31.4 %copy-start.7 = (f32[512]{0:T(512)S(1)}, f32[512]{0:T(512)}, u32[]{:S(2)}) copy-start(f32[512]{0:T(512)} %param.11) | copy-start | bytes 6148
  8.1 77.4 %all-reduce.3.cloned.1.call-start = ((), (), s32[]{:S(2)}) async-start(), calls=%async_computation.4 | async-start | bytes 262144
  11.3 29.6 %copy-start.2 = (bf16[2,1536]{1,0:T(2,128)(2,1)S(1)}, bf16[2,1536]{1,0:T(2,128)(2,1)}, u32[]{:S(2)}) copy-start(bf16[2,1536]{1,0:T(2,128)(2,1)} %param.8) | copy-start | bytes 18436
  11.3 78.9 %reduce-scatter.5.cloned.1.call-start = ((), (), s32[]{:S(2)}) async-start(), calls=%async_computation.3 | async-start | bytes 1310720 | tf_op jit(solution)/shard_map/reduce_scatter | solution.py:44
  39.5 32.4 %copy-start.3 = (f32[1536]{0:T(1024)S(1)}, f32[1536]{0:T(1024)}, u32[]{:S(2)}) copy-start(f32[1536]{0:T(1024)} %param.10) | copy-start | bytes 18436
  39.5 32.4 %copy-start.5 = (bf16[16,384]{1,0:T(8,128)(2,1)S(1)}, bf16[16,384]{1,0:T(8,128)(2,1)}, u32[]{:S(2)}) copy-start(bf16[16,384]{1,0:T(8,128)(2,1)} %param.14) | copy-start | bytes 36868
  40.9 65.2 %reduce-scatter.3.cloned.1.call-start = ((), (), s32[]{:S(2)}) async-start(), calls=%async_computation.2 | async-start | bytes 2949120 | tf_op jit(solution)/shard_map/reduce_scatter | solution.py:43
  73.9 0.7 copy-start.8
Sparse Core Ops, SparseCore 0:
  12.2 73.2 all-reduce.2
Sparse Core Ops, SparseCore 1:
  41.0 24.1 reduce-scatter.4
  74.0 32.0 reduce-scatter.2
where the time goes:
time: 114 us
  blocking collectives  58.7 us (51%)
  waiting for transfers between devices  25.3 us (22%)
  between operations  16.3 us (14%)
  other arithmetic  5.96 us (5%)
  matrix products  4.73 us (4%)
  local copies, waits for them, and re-layouts  2.45 us (2%)
    all_gather x1, blocking collectives, body(): lax.all_gather(query_latent, 'tensor', axis=0, tiled=True)  30.8 us
    all_gather x1, blocking collectives, body(): lax.all_gather(key_value_latent, 'tensor', axis=0, tiled=True)  27.9 us
    reduce_scatter x1, waiting for transfers between devices, body(): lax.psum_scatter(part_q, 'dp', scatter_dimension=0, tiled=True)  15.9 us
    unnamed x4, waiting for transfers between devices  9.45 us
    dot_general x2, matrix products, contract_rows(): lax.dot_general(left, right, (((0,), (0,)), ((), ())), preferred_element_...  3.37 us
    mul x2, other arithmetic, backward_of_norm(): return inverse_norm * (scaled_gradient - unit_input * mean_correction)  2.87 us
    unnamed x19, local copies, waits for them, and re-layouts  2.42 us
  transfers between devices with their start and end apart: 3, of which 2 were waited for; matrix products, arithmetic and copies ran while one was open for 8% of the time, Pallas kernels for 0%

commit v1 on v0

--- a/solution.py
+++ b/solution.py
@@ -34,7 +34,10 @@
 def body(query_latent, key_value_latent, query_gain, key_value_gain, q_up, kv_up, grad_q, grad_kv):
     query_width = query_latent.shape[1]
     whole_q, whole_kv = (
-        lax.all_gather(query_latent, "tensor", axis=0, tiled=True),
+        jnp.concatenate(
+            lax.all_to_all(jnp.stack([query_latent] * lax.axis_size("tensor")), "tensor", 0, 0),
+            axis=0,
+        ),
         lax.all_gather(key_value_latent, "tensor", axis=0, tiled=True),
     )
     part_q = contract_rows(apply_norm(whole_q, query_gain)[2], grad_q)

time: 114 us -> 109 us (0.956)
  blocking collectives: 58.7 us -> 38.5 us
  waiting for transfers between devices: 25.3 us -> 40.2 us
    all_gather x1 -> x0, blocking collectives: 30.8 us -> none  [body(): lax.all_gather(query_latent, 'tensor', axis=0, tiled=True)]
    unnamed x4, waiting for transfers between devices: 9.45 us -> 29.5 us
    all_to_all x0 -> x1, blocking collectives: none -> 10.6 us  [body(): lax.all_to_all(jnp.stack([query_latent] * lax.axis_size('tensor')), 'tens...]
    reduce_scatter x1, waiting for transfers between devices: 15.9 us -> 10.7 us  [body(): lax.psum_scatter(part_q, 'dp', scatter_dimension=0, tiled=True)]
  transfers between devices with their start and end apart: 3 -> 3, of which waited for: 2 -> 2; matrix products, arithmetic and copies ran while one was open for 8% -> 9% of each run, Pallas kernels for 0% -> 0%
where the time goes in v1:
time: 109 us; the launch traced here: 108 us
  waiting for transfers between devices  40.2 us (37%)
  blocking collectives  38.5 us (35%)
  between operations  16.3 us (15%)
  other arithmetic  5.97 us (5%)
  matrix products  4.73 us (4%)
  local copies, waits for them, and re-layouts  2.56 us (2%)
    unnamed x4, waiting for transfers between devices  29.5 us
    all_gather x1, blocking collectives, body(): lax.all_gather(key_value_latent, 'tensor', axis=0, tiled=True)  27.9 us
    reduce_scatter x1, waiting for transfers between devices, body(): lax.psum_scatter(part_q, 'dp', scatter_dimension=0, tiled=True)  10.7 us
    all_to_all x1, blocking collectives, body(): lax.all_to_all(jnp.stack([query_latent] * lax.axis_size('tensor')), 'tens...  10.6 us
    dot_general x2, matrix products, contract_rows(): lax.dot_general(left, right, (((0,), (0,)), ((), ())), preferred_element_...  3.37 us
    mul x2, other arithmetic, backward_of_norm(): return inverse_norm * (scaled_gradient - unit_input * mean_correction)  2.87 us
    unnamed x19, local copies, waits for them, and re-layouts  2.43 us
  transfers between devices with their start and end apart: 3, of which 2 were waited for; matrix products, arithmetic and copies ran while one was open for 9% of the time, Pallas kernels for 0%

profile of v1, /device:TPU:0, one launch (start us, length us, event | category | flops | bytes accessed | tf_op | source)
XLA Modules:
  0.0 108.4 jit_solution(14065719198789259860)
XLA Ops:
  8.0 0.0 copy-start
  8.1 0.0 all-reduce.3.cloned.1.call-start
  8.1 1.2 %copy-done = bf16[1536,384]{1,0:T(8,128)(2,1)S(1)} copy-done((bf16[1536,384]{1,0:T(8,128)(2,1)S(1)}, bf16[1536,384]{1,0:T(8,128)(2,1)}, u32[]{:S(2)}) %copy-start) | copy-done | bytes 1179672
  9.3 1.1 %fusion.18 = f32[16,1536]{1,0:T(8,128)S(1)} fusion(bf16[16,384]{1,0:T(8,128)(2,1)} %param.14, bf16[1536,384]{1,0:T(8,128)(2,1)S(1)} %copy-done), kind=kOutput, calls=%fused_computation.35 | convolution fusion | flops 18874368 | bytes 1290240 | tf_op jit(solution)/shard_map/dot_general | solution.py:29
  10.4 0.0 copy-done.4
  10.4 0.3 fusion.19
  10.6 0.7 pad_maximum_fusion
  11.3 0.0 all-reduce.3.cloned.1.call-update
  11.3 0.0 reduce-scatter.5.cloned.1.call-start
  11.4 27.9 %all-gather = bf16[8,2,512]{2,1,0:T(2,128)(2,1)S(1)} all-gather(bf16[1,2,512]{2,1,0:T(2,128)(2,1)S(1)} %bitcast.8), channel_id=1, replica_groups=mesh['dp'=4,'tensor'=8] {'tensor'}, dimensions={0}, use_global_device_ids=true | all-gather | bytes 18432 | tf_op jit(solution)/shard_map/all_gather | solution.py:41
  39.3 0.1 multiply_reduce_fusion.1
  39.5 0.0 copy-done.7
  39.5 0.0 copy-start.3
  39.5 0.0 copy-start.5
  39.5 1.4 %fusion.3 = f32[512,512]{1,0:T(8,128)} fusion(bf16[16,512]{1,0:T(8,128)(2,1)S(1)} %copy-done.4, f32[16,512]{1,0:T(8,128)S(1)} %reshape.67, f32[16]{0:T(128)S(1)} %add_rsqrt_fusion.1, f32[512]{0:T(512)S(1)} %copy-done.7), kind=kOutput, calls=%fused_computation.8 | convolution fusion | flops 8413184 | bytes 1099840 | tf_op jit(solution)/shard_map/dot_general | solution.py:23
  40.9 0.0 reduce-scatter.5.cloned.1.call-update
  40.9 0.0 reduce-scatter.3.cloned.1.call-start
  41.0 10.6 %all_to_all.5 = bf16[8,2,1536]{2,1,0:T(2,128)(2,1)S(1)} all-to-all(bf16[8,2,1536]{2,1,0:T(2,128)(2,1)S(1)} %stack.2), channel_id=1, replica_groups=mesh['dp'=4,'tensor'=8] {'tensor'}, dimensions={0} | all-to-all | bytes 98304 | tf_op jit(solution)/shard_map/all_to_all | solution.py:38
  51.6 0.1 multiply_reduce_fusion
  51.7 0.1 rsqrt.38
  51.8 2.0 %fusion = f32[1536,384]{1,0:T(8,128)} fusion(bf16[16,384]{1,0:T(8,128)(2,1)S(1)} %copy-done.5, f32[16,1536]{1,0:T(8,128)S(1)} %reshape.64, f32[16]{0:T(128)S(1)} %rsqrt.38, f32[1536]{0:T(1024)S(1)} %copy-done.3), kind=kOutput, calls=%fused_computation.3 | convolution fusion | flops 18948096 | bytes 2476096 | tf_op jit(solution)/shard_map/dot_general | solution.py:23
  53.8 0.0 reduce-scatter.3.cloned.1.call-update
  53.9 0.6 copy-done.8
  54.5 0.6 dynamic-slice
  55.7 0.1 fusion.17
  55.8 0.1 fusion.11
  56.0 29.5 %all-reduce.3.cloned.1.call-done = f32[16,2048]{1,0:T(8,128)} async-done(((f32[16,2048]{1,0:T(8,128)}), f32[16,2048]{1,0:T(8,128)}) %all-reduce.3.cloned.1.call-update) | async-done | bytes 131088
  85.5 0.9 fusion.14
  86.4 1.0 fusion.8
  87.4 1.4 %fusion.16 = f32[2,512]{1,0:T(2,128)} fusion(bf16[2,512]{1,0:T(2,128)(2,1)S(1)} %copy-done.6, f32[2]{0:T(128)S(1)} %broadcast_multiply_fusion, f32[2]{0:T(128)S(1)} %add_rsqrt_fusion.2, f32[16,2048]{1,0:T(8,128)} %all-reduce.3.cloned.1.call-done, u32[]{:T(128)S(6)} %multiply.38, u32[]{:T(128)S(6)} %convert.1, f32[512]{0:T(512)S(1)} %copy-done.7), kind=kLoop, calls=%fused_computation.26 | loop fusion | flops 6144 | bytes 12312 | tf_op jit(solution)/shard_map/mul | solution.py:19
  88.8 1.5 %fusion.10 = f32[2,1536]{1,0:T(2,128)} fusion(bf16[2,1536]{1,0:T(2,128)(2,1)S(1)} %copy-done.2, f32[16,2048]{1,0:T(8,128)} %all-reduce.3.cloned.1.call-done, u32[]{:T(128)S(6)} %multiply.38, f32[2]{0:T(128)S(1)} %broadcast_multiply_fusion.1, f32[2]{0:T(128)S(1)} %add_rsqrt_fusion.3, f32[1536]{0:T(1024)S(1)} %copy-done.3), kind=kLoop, calls=%fused_computation.17 | loop fusion | flops 18432 | bytes 36884 | tf_op jit(solution)/shard_map/mul | solution.py:19
  90.3 10.7 %reduce-scatter.3.cloned.1.call-done = f32[384,384]{1,0:T(8,128)} async-done(((f32[1536,384]{1,0:T(8,128)}), f32[384,384]{1,0:T(8,128)}) %reduce-scatter.3.cloned.1.call-update) | async-done | bytes 589840 | tf_op jit(solution)/shard_map/reduce_scatter | solution.py:46
  (21 shorter events, 0.1 us)
Async XLA Ops:
  8.0 1.3 %copy-start = (bf16[1536,384]{1,0:T(8,128)(2,1)S(1)}, bf16[1536,384]{1,0:T(8,128)(2,1)}, u32[]{:S(2)}) copy-start(bf16[1536,384]{1,0:T(8,128)(2,1)} %param.12) | copy-start | bytes 3538948
  8.0 2.4 %copy-start.1 = (bf16[512,512]{1,0:T(8,128)(2,1)S(1)}, bf16[512,512]{1,0:T(8,128)(2,1)}, u32[]{:S(2)}) copy-start(bf16[512,512]{1,0:T(8,128)(2,1)} %param.13) | copy-start | bytes 1572868
  8.0 2.4 %copy-start.4 = (bf16[16,512]{1,0:T(8,128)(2,1)S(1)}, bf16[16,512]{1,0:T(8,128)(2,1)}, u32[]{:S(2)}) copy-start(bf16[16,512]{1,0:T(8,128)(2,1)} %param.15) | copy-start | bytes 49156
  8.0 3.4 %copy-start.6 = (bf16[2,512]{1,0:T(2,128)(2,1)S(1)}, bf16[2,512]{1,0:T(2,128)(2,1)}, u32[]{:S(2)}) copy-start(bf16[2,512]{1,0:T(2,128)(2,1)} %param.9) | copy-start | bytes 6148
  8.0 31.4 %copy-start.7 = (f32[512]{0:T(512)S(1)}, f32[512]{0:T(512)}, u32[]{:S(2)}) copy-start(f32[512]{0:T(512)} %param.11) | copy-start | bytes 6148
  8.1 77.4 %all-reduce.3.cloned.1.call-start = ((), (), s32[]{:S(2)}) async-start(), calls=%async_computation.5 | async-start | bytes 262144
  11.3 29.6 %copy-start.2 = (bf16[2,1536]{1,0:T(2,128)(2,1)S(1)}, bf16[2,1536]{1,0:T(2,128)(2,1)}, u32[]{:S(2)}) copy-start(bf16[2,1536]{1,0:T(2,128)(2,1)} %param.8) | copy-start | bytes 18436
  11.3 78.9 %reduce-scatter.5.cloned.1.call-start = ((), (), s32[]{:S(2)}) async-start(), calls=%async_computation.4 | async-start | bytes 1310720 | tf_op jit(solution)/shard_map/reduce_scatter | solution.py:47
  39.5 12.3 %copy-start.3 = (f32[1536]{0:T(1024)S(1)}, f32[1536]{0:T(1024)}, u32[]{:S(2)}) copy-start(f32[1536]{0:T(1024)} %param.10) | copy-start | bytes 18436
  39.5 12.3 %copy-start.5 = (bf16[16,384]{1,0:T(8,128)(2,1)S(1)}, bf16[16,384]{1,0:T(8,128)(2,1)}, u32[]{:S(2)}) copy-start(bf16[16,384]{1,0:T(8,128)(2,1)} %param.14) | copy-start | bytes 36868
  40.9 60.0 %reduce-scatter.3.cloned.1.call-start = ((), (), s32[]{:S(2)}) async-start(), calls=%async_computation.3 | async-start | bytes 2949120 | tf_op jit(solution)/shard_map/reduce_scatter | solution.py:46
  53.8 0.7 copy-start.8
Sparse Core Ops, SparseCore 0:
  12.2 73.2 all-reduce.2
Sparse Core Ops, SparseCore 1:
  41.0 24.1 reduce-scatter.4
  68.2 32.7 reduce-scatter.2
